TPU v7x, 32 devices: a whole 2x2x4 slice. The times are simulated.
32 devices in a mesh: grp: 2 (over y), theta: 8 (over z, x), phi: 2 (over core).
Axes of the slice: x: 2, y: 2, z: 4, core: 2. Of those that a mesh axis runs over, the one named last changes fastest.
Arguments:
- maps: bfloat16 [8, 4096, 4096], P('grp', 'theta', 'phi'), parts along dimension 0, may hold values from -6 to 6
- deltas: bfloat16 [4096, 4, 4096], P('phi', None, 'theta'), may hold values from -1 to 1
- spin_rows: bfloat16 [4096, 2, 4], P('phi'), may hold values from -1 to 1
- ell_index: int32 [4], replicated, may hold values from 1024 to 2047
- owner_map: int32 [4096], replicated, may hold values from 0 to 4095, each once
- prior: float32 [4], replicated, may hold values from 0.3 to 3
Outputs:
- gradient: float32 [8, 2, 4096], P('grp', None, ('theta', 'phi')), parts along dimension 0
There are 2 independent parts, one for each index of `grp`. A program takes and returns all parts, laid end to end along the dimension named above; an argument that names none is the same for every part. Nothing has to cross between parts.
Inputs may be any that keep to these rules, and one draw needn't show every extreme that they name: `ell_index`: every selected degree is at least 1024; tables may repeat a degree. A permutation of the Fourier indices; slot s of deltas and of the output belongs to the frequency owner_map[s].
All inputs are finite; a program needn't handle non-finite values.
Results may differ from a plain program's by a relative error of at most 0.0003.
Values may be sent and summed in bfloat16 or wider, within the bound.
A program may use at most 256 MiB of HBM per device.

v0:
```python
import math

import jax
import jax.numpy as jnp
from jax import lax
from jax.sharding import PartitionSpec as P


def exact_einsum(form, table, operand):
    return jnp.einsum(form, table, operand, precision=lax.Precision.HIGHEST)


def angle_tables(row_count, start, count, modulus):
    freq_rows = jnp.arange(row_count, dtype=jnp.int32)
    sample_cols = start + jnp.arange(count, dtype=jnp.int32)
    angles = (
        2.0
        * math.pi
        / modulus
        * jnp.mod(freq_rows[:, None] * sample_cols[None, :], modulus).astype(jnp.float32)
    )
    return (jnp.cos(angles), jnp.sin(angles))


def row_transform(real_part, imag_part, outer_len, inner_len):
    row_count = real_part.shape[0]
    length = outer_len * inner_len
    cos_a, sin_a = angle_tables(outer_len, 0, outer_len, outer_len)
    real_blocks = real_part.reshape(row_count, outer_len, inner_len)
    section_real = exact_einsum("ka,rab->rkb", cos_a, real_blocks)
    section_imag = -exact_einsum("ka,rab->rkb", sin_a, real_blocks)
    if imag_part is not None:
        imag_blocks = imag_part.reshape(row_count, outer_len, inner_len)
        section_real = section_real + exact_einsum("ka,rab->rkb", sin_a, imag_blocks)
        section_imag = section_imag + exact_einsum("ka,rab->rkb", cos_a, imag_blocks)
    cos_t, sin_t = angle_tables(outer_len, 0, inner_len, length)
    turned_real = section_real * cos_t + section_imag * sin_t
    turned_imag = section_imag * cos_t - section_real * sin_t
    cos_b, sin_b = angle_tables(inner_len, 0, inner_len, inner_len)
    out_real = exact_einsum("qb,rkb->rqk", cos_b, turned_real) + exact_einsum(
        "qb,rkb->rqk", sin_b, turned_imag
    )
    out_imag = exact_einsum("qb,rkb->rqk", cos_b, turned_imag) - exact_einsum(
        "qb,rkb->rqk", sin_b, turned_real
    )
    return (out_real.reshape(row_count, length), out_imag.reshape(row_count, length))


def column_transform(real_part, imag_part, outer_len, inner_len, start):
    fields = real_part.shape[0]
    count = real_part.shape[2]
    slots = real_part.shape[3]
    length = outer_len * inner_len
    cos_a, sin_a = angle_tables(outer_len, 0, outer_len, outer_len)
    section_real = exact_einsum("ka,fabm->fkbm", cos_a, real_part) + exact_einsum(
        "ka,fabm->fkbm", sin_a, imag_part
    )
    section_imag = exact_einsum("ka,fabm->fkbm", cos_a, imag_part) - exact_einsum(
        "ka,fabm->fkbm", sin_a, real_part
    )
    cos_t, sin_t = angle_tables(outer_len, start, count, length)
    cos_t = cos_t[:, :, None]
    sin_t = sin_t[:, :, None]
    turned_real = section_real * cos_t + section_imag * sin_t
    turned_imag = section_imag * cos_t - section_real * sin_t
    cos_b, sin_b = angle_tables(inner_len, start, count, inner_len)
    out_real = exact_einsum("qb,fkbm->fqkm", cos_b, turned_real) + exact_einsum(
        "qb,fkbm->fqkm", sin_b, turned_imag
    )
    out_imag = exact_einsum("qb,fkbm->fqkm", cos_b, turned_imag) - exact_einsum(
        "qb,fkbm->fqkm", sin_b, turned_real
    )
    return (out_real.reshape(fields, length, slots), out_imag.reshape(fields, length, slots))


def accumulate(spectrum_block, table_block, spin_block, length, ell_index):
    count = table_block.shape[0]
    positions = jnp.arange(count, dtype=jnp.int32)
    freq = jnp.where(positions < length // 2, positions, positions - length)
    terms = []
    for degree in range(table_block.shape[1]):
        keep_rows = (jnp.abs(freq) <= ell_index[degree]).astype(jnp.float32)
        row_weights = spin_block[:, :, degree].astype(jnp.float32).T * keep_rows[None, :]
        table = table_block[:, degree, :].astype(jnp.float32)
        terms.append(
            jnp.einsum(
                "fk,ks,xfks->fxs",
                row_weights,
                table,
                spectrum_block,
                precision=lax.Precision.HIGHEST,
            )
        )
    return jnp.stack(terms)


def on_device(maps, deltas, spin_rows, ell_index, owner_map, prior):
    theta_count = lax.axis_size("theta")
    phi_count = lax.axis_size("phi")
    length = maps.shape[2] * phi_count
    values = maps.astype(jnp.float32)
    planes = jnp.stack([values[0], values[1] * values[2], values[1] * values[3]])
    row_planes = lax.all_to_all(planes, "phi", split_axis=1, concat_axis=2, tiled=True)
    inner_len = length // theta_count
    spectra = [
        row_transform(row_planes[0], None, theta_count, inner_len),
        row_transform(row_planes[1], row_planes[2], theta_count, inner_len),
    ]
    stacked = jnp.stack(
        [
            jnp.stack([spectrum[0] for spectrum in spectra]),
            jnp.stack([spectrum[1] for spectrum in spectra]),
        ]
    )
    permuted = jnp.take(stacked, owner_map, axis=3)
    columns = lax.all_to_all(permuted, "theta", split_axis=3, concat_axis=2, tiled=True)
    fields = columns.shape[1]
    slots = columns.shape[3]
    sub_rows = columns.shape[2] // theta_count
    blocks = columns.reshape(2, fields, theta_count, sub_rows, slots)
    row_start = lax.axis_index("phi") * sub_rows
    spec_real, spec_imag = column_transform(blocks[0], blocks[1], theta_count, inner_len, row_start)
    combined = jnp.stack([spec_real, spec_imag])
    totals = accumulate(
        combined,
        lax.all_gather(deltas, "phi", axis=0, tiled=True),
        lax.all_gather(spin_rows, "phi", axis=0, tiled=True),
        length,
        ell_index,
    )
    shares = lax.psum_scatter(totals, "phi", scatter_dimension=3, tiled=True)
    share_count = shares.shape[3]
    slot_start = lax.axis_index("theta") * slots + lax.axis_index("phi") * share_count
    share_ids = lax.dynamic_slice_in_dim(owner_map, slot_start, share_count)
    slot_freq = jnp.where(share_ids < length // 2, share_ids, share_ids - length)
    ell_float = ell_index.astype(jnp.float32)
    weight = 2.0 * math.pi / length * jnp.sqrt((2.0 * ell_float + 1.0) / (4.0 * math.pi)) / length
    keep_slots = (jnp.abs(slot_freq)[None, :] <= ell_index[:, None]).astype(jnp.float32) * weight[
        :, None
    ]
    scalar_real = shares[:, 0, 0] * keep_slots
    scalar_imag = shares[:, 0, 1] * keep_slots
    spin_real = shares[:, 1, 0] * keep_slots
    spin_imag = shares[:, 1, 1] * keep_slots
    coupling = (prior * jnp.sqrt(ell_float * (ell_float + 1.0)) / (length // 2))[:, None]
    inner_real = -spin_imag - coupling * scalar_real
    inner_imag = spin_real - coupling * scalar_imag
    turns = jnp.mod(-slot_freq, 4)
    phase_real = jnp.where(turns == 0, 1.0, jnp.where(turns == 2, -1.0, 0.0)).astype(jnp.float32)[
        None, :
    ]
    phase_imag = jnp.where(turns == 1, 1.0, jnp.where(turns == 3, -1.0, 0.0)).astype(jnp.float32)[
        None, :
    ]
    out_real = phase_real * inner_real - phase_imag * inner_imag
    out_imag = phase_real * inner_imag + phase_imag * inner_real
    return jnp.stack([out_real, out_imag], axis=1)


def solution(mesh):
    placed = (
        P("grp", "theta", "phi"),
        P("phi", None, "theta"),
        P("phi", None, None),
        P(),
        P(),
        P(),
    )
    return jax.shard_map(
        on_device,
        mesh=mesh,
        in_specs=placed,
        out_specs=P("grp", None, ("theta", "phi")),
        check_vma=False,
    )
```

profile of v0, /device:TPU:0, one launch (start us, length us, event | category | flops | bytes accessed | tf_op | source)
XLA Modules:
  0.0 1105.6 jit_solution(13020259938788177995)
XLA Ops:
  6.5 11.3 %convert_element_type.145 = f32[4,512,2048]{2,1,0:T(8,128)} convert(bf16[4,512,2048]{2,1,0:T(8,128)(2,1)} %param.6) | non-fusion elementwise | flops 4194304 | bytes 25165824 | tf_op jit(solution)/shard_map/convert_element_type | solution.py:101
  22.0 8.4 slice_multiply_fusion.1
  30.3 9.8 pad_maximum_fusion.1
  40.1 16.7 %copy.115 = f32[3,512,2048]{2,0,1:T(4,128)S(1)} copy(f32[3,512,2048]{2,1,0:T(8,128)} %pad_maximum_fusion.1) | data formatting | bytes 25165824 | tf_op jit(solution)/shard_map/stack | solution.py:102
  56.8 17.4 %all_to_all.30 = f32[3,512,2048]{2,0,1:T(4,128)S(1)} all-to-all(f32[3,512,2048]{2,0,1:T(4,128)S(1)} %copy.115), channel_id=1, replica_groups=mesh['grp'=2,'theta'=8,'phi'=2] {'phi'}, dimensions={1} | all-to-all | bytes 25165824 | tf_op jit(solution)/shard_map/all_to_all | solution.py:103
  74.2 14.4 %copy.241 = f32[3,2,256,2048]{3,1,2,0:T(2,128)} copy(f32[3,2,256,2048]{3,0,2,1:T(4,128)S(1)} %bitcast.262) | data formatting | bytes 25165824 | tf_op jit(solution)/shard_map/all_to_all | solution.py:103
  88.6 8.9 fusion.248
  104.0 8.7 fusion.126
  124.7 10.2 negate_add_fusion
  146.8 8.6 fusion.129
  155.5 10.5 fusion.24
  166.0 13.1 %fusion.36 = f32[256,8,512]{2,0,1:T(8,128)S(1)} fusion(f32[256,8,512]{2,1,0:T(8,128)S(1)} %get-tuple-element.26), kind=kOutput, calls=%fused_computation.77 | convolution fusion | flops 6446120960 | bytes 8388608 | tf_op jit(solution)/shard_map/qb,rkb->rqk/dot_general | solution.py:10
  179.0 15.6 %fusion.34 = f32[256,8,512]{2,0,1:T(8,128)} fusion(f32[256,8,512]{2,1,0:T(8,128)S(1)} %get-tuple-element.26), kind=kOutput, calls=%fused_computation.75 | convolution fusion | flops 6446120960 | bytes 8388608 | tf_op jit(solution)/shard_map/qb,rkb->rqk/dot_general | solution.py:10
  194.6 15.8 %fusion.28 = f32[256,8,512]{2,0,1:T(8,128)} fusion(f32[256,8,512]{2,1,0:T(8,128)S(1)} %get-tuple-element.37), kind=kOutput, calls=%fused_computation.69 | convolution fusion | flops 6446120960 | bytes 8388608 | tf_op jit(solution)/shard_map/qb,rkb->rqk/dot_general | solution.py:10
  210.4 16.0 %fusion.26 = f32[256,8,512]{2,0,1:T(8,128)} fusion(f32[256,8,512]{2,1,0:T(8,128)S(1)} %get-tuple-element.37), kind=kOutput, calls=%fused_computation.67 | convolution fusion | flops 6446120960 | bytes 8388608 | tf_op jit(solution)/shard_map/qb,rkb->rqk/dot_general | solution.py:10
  226.5 15.9 %add_bitcast_fusion.2 = f32[256,512,8]{1,0,2:T(8,128)} fusion(f32[256,8,512]{2,0,1:T(8,128)S(1)} %fusion.36, f32[256,8,512]{2,1,0:T(8,128)S(1)} %get-tuple-element.25), kind=kOutput, calls=%fused_computation.66 | convolution fusion | flops 6447169536 | bytes 12582912 | tf_op jit(solution)/shard_map/qb,rkb->rqk/dot_general | solution.py:10
  247.8 9.5 copy.123
  257.3 15.8 %add_bitcast_fusion.1 = f32[256,512,8]{1,0,2:T(8,128)} fusion(f32[256,8,512]{2,0,1:T(8,128)S(1)} %copy-done.13, f32[256,8,512]{2,1,0:T(8,128)S(1)} %copy-done.4), kind=kOutput, calls=%fused_computation.64 | convolution fusion | flops 6447169536 | bytes 12582912 | tf_op jit(solution)/shard_map/qb,rkb->rqk/dot_general | solution.py:10
  278.6 9.5 copy.124
  288.1 16.1 %subtract_bitcast_fusion.2 = f32[256,512,8]{1,0,2:T(8,128)} fusion(f32[256,8,512]{2,0,1:T(8,128)S(1)} %copy-done.12, f32[256,8,512]{2,1,0:T(8,128)S(1)} %copy-done.7), kind=kOutput, calls=%fused_computation.63 | convolution fusion | flops 6447169536 | bytes 12582912 | tf_op jit(solution)/shard_map/qb,rkb->rqk/dot_general | solution.py:10
  309.7 9.5 copy.131
  319.1 15.8 %subtract_bitcast_fusion.1 = f32[256,512,8]{1,0,2:T(8,128)} fusion(f32[256,8,512]{2,0,1:T(8,128)S(1)} %copy-done.11, f32[256,8,512]{2,1,0:T(8,128)S(1)} %copy-done.5), kind=kOutput, calls=%fused_computation.62 | convolution fusion | flops 6447169536 | bytes 12582912 | tf_op jit(solution)/shard_map/qb,rkb->rqk/dot_general | solution.py:10
  340.4 7.9 copy.132
  363.8 8.6 pad_maximum_fusion
  372.4 52.5 %gather_fusion = f32[4096,2,2,256]{3,2,1,0:T(2,128)} fusion(f32[2,2,256,4096]{2,1,3,0:T(2,128)} %pad_maximum_fusion, s32[4096]{0:T(1024)S(1)} %fusion.105), kind=kCustom, calls=%fused_computation | custom fusion | bytes 33570816 | tf_op jit(solution)/shard_map/jit(_take)/gather | solution.py:115
  424.9 17.6 %select_bitcast_fusion = f32[2,2,256,4096]{2,1,0,3:T(2,128)} fusion(f32[4096,2,2,256]{3,2,1,0:T(2,128)} %gather_fusion, pred[4096]{0:T(1024)(128)(4,1)S(1)} %compare_and_fusion), kind=kLoop, calls=%fused_computation.9 | loop fusion | flops 4194304 | bytes 33558528 | tf_op jit(solution)/shard_map/jit(_take)/select_n | solution.py:115
  449.8 8.4 copy.114
  472.9 17.0 %all-gather.2.cloned.1.call-done = bf16[4096,4,512]{2,0,1:T(8,128)(2,1)} async-done(((bf16[2048,4,512]{2,0,1:T(8,128)(2,1)}), bf16[4096,4,512]{2,0,1:T(8,128)(2,1)}) %all-gather.2.cloned.1.call-update) | async-done | bytes 16777232 | tf_op jit(solution)/shard_map/all_gather | solution.py:126
  489.9 15.4 %fusion.18 = (f32[4096,512]{1,0:T(8,128)}, f32[4096,512]{1,0:T(8,128)}, f32[4096,512]{1,0:T(8,128)}, f32[4096,512]{1,0:T(8,128)}) fusion(bf16[4096,4,512]{2,0,1:T(8,128)(2,1)} %all-gather.2.cloned.1.call-done), kind=kLoop, calls=%fused_computation.41 | loop fusion | flops 8388608 | bytes 50331648 | tf_op jit(solution)/shard_map/convert.15
  505.3 20.2 %multiply_bitcast_fusion = (f32[2,512,4096]{1,0,2:T(2,128)}, f32[2,512,4096]{1,0,2:T(2,128)}) fusion(f32[4096,512]{1,0:T(8,128)} %get-tuple-element.16, f32[4096,2]{1,0:T(8,128)} %copy.144, f32[4096,512]{1,0:T(8,128)} %get-tuple-element.17, f32[4096,2]{1,0:T(8,128)S(1)} %copy.143), kind=kLoop, calls=%fused_computation.10 | loop fusion | flops 8388608 | bytes 50397184
  525.4 15.2 %copy.190 = f32[2,512,4096]{1,2,0:T(8,128)} copy(f32[2,512,4096]{1,0,2:T(2,128)} %get-tuple-element.48) | data formatting | bytes 33554432
  541.9 8.9 copy.191
  550.8 20.1 %multiply_bitcast_fusion.2 = (f32[2,512,4096]{1,0,2:T(2,128)}, f32[2,512,4096]{1,0,2:T(2,128)}) fusion(f32[4096,512]{1,0:T(8,128)} %get-tuple-element.18, f32[4096,2]{1,0:T(8,128)} %copy.142, f32[4096,512]{1,0:T(8,128)} %get-tuple-element.19, f32[4096,2]{1,0:T(8,128)S(1)} %copy-done.18), kind=kLoop, calls=%fused_computation.12 | loop fusion | flops 8388608 | bytes 50397184
  571.0 15.2 %copy.188 = f32[2,512,4096]{1,2,0:T(8,128)} copy(f32[2,512,4096]{1,0,2:T(2,128)} %get-tuple-element.50) | data formatting | bytes 33554432
  587.4 8.8 copy.189
  596.3 216.9 %all-to-all-done.1 = f32[2,2,256,4096]{2,1,0,3:T(2,128)} async-done(((f32[2,2,256,4096]{2,1,0,3:T(2,128)}), f32[2,2,256,4096]{2,1,0,3:T(2,128)}, u32[]{:S(2)}, u32[]{:S(2)}) %all-to-all-start.1) | async-done | bytes 16777248 | tf_op jit(solution)/shard_map/all_to_all | solution.py:116
  813.2 19.4 %copy.177 = f32[2,2,256,8,512]{4,3,2,1,0:T(8,128)} copy(f32[2,2,256,8,512]{2,1,0,4,3:T(2,128)} %bitcast.33) | data formatting | bytes 33554432 | tf_op jit(solution)/shard_map/all_to_all | solution.py:116
  832.6 11.8 %fusion.2 = f32[2,256,512,8]{2,3,1,0:T(8,128)} fusion(f32[2,2,8,256,512]{4,2,3,1,0:T(8,128)} %bitcast.258), kind=kOutput, calls=%fused_computation.28 | convolution fusion | flops 201327488 | bytes 16777216 | tf_op jit(solution)/shard_map/ka,fabm->fkbm/dot_general | solution.py:10
  844.4 9.4 fusion.3
  853.8 9.4 fusion.5
  863.2 21.9 %fusion = (f32[2,8,256,512]{3,1,2,0:T(8,128)}, f32[2,8,256,512]{3,1,2,0:T(8,128)}) fusion(f32[8,256]{0,1:T(8,128)S(1)} %copy.135, f32[8,256]{0,1:T(8,128)S(1)} %copy.134, f32[2,256,512,8]{2,3,1,0:T(8,128)} %fusion.2, f32[2,256,512,8]{2,3,1,0:T(8,128)} %fusion.3, f32[2,256,512,8]{2,3,1,0:T(8,128)} %fusion.5, f32[2,2,8,256,512]{4,2,3,1,0:T(8,128)} %bitcast.259), kind=kOutput, calls=%fused_computation.24 | convolution fusion | flops 218104704 | bytes 50348032 | tf_op jit(solution)/shard_map/ka,fabm->fkbm/dot_general | solution.py:10
  885.1 26.0 %fusion.8 = f32[2,8,512,512]{2,3,1,0:T(8,128)} fusion(f32[2,8,256,512]{3,1,2,0:T(8,128)} %get-tuple-element.15, s32[256]{0:T(256)S(1)} %iota_add_fusion), kind=kOutput, calls=%fused_computation.34 | convolution fusion | flops 12886736896 | bytes 25166848 | tf_op jit(solution)/shard_map/qb,fkbm->fqkm/dot_general | solution.py:10
  911.1 25.8 %fusion.6 = f32[2,8,512,512]{2,3,1,0:T(8,128)S(1)} fusion(f32[2,8,256,512]{3,1,2,0:T(8,128)} %get-tuple-element.15, s32[256]{0:T(256)S(1)} %iota_add_fusion), kind=kOutput, calls=%fused_computation.32 | convolution fusion | flops 12886736896 | bytes 25166848 | tf_op jit(solution)/shard_map/qb,fkbm->fqkm/dot_general | solution.py:10
  936.9 49.7 %add_bitcast_fusion = f32[2,512,8,512]{3,1,2,0:T(8,128)} fusion(f32[2,8,512,512]{2,3,1,0:T(8,128)} %fusion.8, f32[2,8,256,512]{3,1,2,0:T(8,128)} %get-tuple-element.14, s32[256]{0:T(256)S(1)} %iota_add_fusion), kind=kOutput, calls=%fused_computation.14 | convolution fusion | flops 12890931200 | bytes 41944064 | tf_op jit(solution)/shard_map/qb,fkbm->fqkm/dot_general | solution.py:10
  986.6 17.7 %copy.240 = f32[2,512,8,512]{3,2,1,0:T(8,128)} copy(f32[2,512,8,512]{3,1,2,0:T(8,128)} %add_bitcast_fusion) | data formatting | bytes 33554432 | tf_op jit(solution)/shard_map/add | solution.py:67
  1004.4 27.7 %subtract_bitcast_fusion = f32[2,512,8,512]{3,1,2,0:T(8,128)} fusion(f32[2,8,512,512]{2,3,1,0:T(8,128)S(1)} %fusion.6, f32[2,8,256,512]{3,1,2,0:T(8,128)} %get-tuple-element.14, s32[256]{0:T(256)S(1)} %iota_add_fusion), kind=kOutput, calls=%fused_computation.13 | convolution fusion | flops 12890931200 | bytes 41944064 | tf_op jit(solution)/shard_map/qb,fkbm->fqkm/dot_general | solution.py:10
  1032.1 19.3 %copy.239 = f32[2,512,8,512]{3,2,1,0:T(8,128)} copy(f32[2,512,8,512]{3,1,2,0:T(8,128)} %subtract_bitcast_fusion) | data formatting | bytes 33554432 | tf_op jit(solution)/shard_map/sub | solution.py:70
  1051.5 27.6 %multiply_reduce_fusion.3 = (f32[2,512,2]{1,0,2:T(2,128)S(1)}, f32[2,512,2]{1,0,2:T(2,128)S(1)}, f32[2,512,2]{1,0,2:T(2,128)S(1)}, f32[2,512,2]{1,0,2:T(2,128)S(1)}) fusion(f32[2,512,4096]{1,2,0:T(8,128)} %copy.188, f32[1,2,4096,512]{3,2,1,0:T(8,128)} %bitcast.264, f32[1,2,4096,512]{3,2,1,0:T(8,128)S(1)} %bitcast.263, f32[2,512,4096]{1,2,0:T(8,128)} %copy.189, ...), kind=kLoop, calls=%fused_computation.5 | loop fusion | flops 75489280 | bytes 100696064 | tf_op jit(solution)/shard_map/fk,ks,xfks->fxs/dot_general | solution.py:86
  (112 shorter events, 115.7 us)
Async XLA Ops:
  104.0 8.7 copy-start.10
  124.7 10.2 copy-start.8
  124.7 10.2 copy-start.14
  146.8 8.6 copy-start.9
  165.9 60.5 %copy-start.6 = (f32[256,8,512]{2,1,0:T(8,128)}, f32[256,8,512]{2,1,0:T(8,128)S(1)}, u32[]{:S(2)}) copy-start(f32[256,8,512]{2,1,0:T(8,128)S(1)} %get-tuple-element.25) | copy-start | bytes 12582916
  194.6 31.8 %copy-start.19 = (s32[4096]{0:T(1024)S(1)}, s32[4096]{0:T(1024)}, u32[]{:S(2)}) copy-start(s32[4096]{0:T(1024)} %param.10) | copy-start | bytes 49156
  247.8 9.5 copy-start.4
  247.8 9.5 copy-start.13
  278.6 9.5 copy-start.7
  278.6 9.5 copy-start.12
  309.6 9.5 copy-start.5
  309.6 9.5 copy-start.11
  340.4 7.9 copy-start.15
  340.4 7.9 copy-start.16
  348.3 7.7 copy-start.17
  442.5 370.7 %all-to-all-start.1 = ((f32[2,2,256,4096]{2,1,0,3:T(2,128)}), f32[2,2,256,4096]{2,1,0,3:T(2,128)}, u32[]{:S(2)}, u32[]{:S(2)}) async-start(f32[2,2,256,4096]{2,1,0,3:T(2,128)} %select_bitcast_fusion), calls=%async_computation.1 | async-start | bytes 33554432 | tf_op jit(solution)/shard_map/all_to_all | solution.py:116
  449.8 40.1 %all-gather.2.cloned.1.call-start = ((), (), s32[]{:S(2)}) async-start(), calls=%async_computation.3 | async-start | bytes 25165824 | tf_op jit(solution)/shard_map/all_gather | solution.py:126
  458.2 0.8 copy-start.20
  458.2 2.6 copy-start.21
  458.2 14.1 %copy-start.27 = (f32[4]{0:T(128)S(1)}, f32[4]{0:T(128)}, u32[]{:S(2)}) copy-start(f32[4]{0:T(128)} %param.11) | copy-start | bytes 52
  458.3 632.6 %reduce-scatter.4.cloned.1.call-start = ((), (), s32[]{:S(2)}) async-start(), calls=%async_computation.4 | async-start | bytes 393216
  525.4 16.5 %copy-start.1 = (f32[2,512,4096]{1,0,2:T(2,128)S(1)}, f32[2,512,4096]{1,0,2:T(2,128)}, u32[]{:S(2)}) copy-start(f32[2,512,4096]{1,0,2:T(2,128)} %get-tuple-element.47) | copy-start | bytes 50331652
  541.9 8.9 copy-start.18
  570.9 16.5 %copy-start.2 = (f32[2,512,4096]{1,0,2:T(2,128)S(1)}, f32[2,512,4096]{1,0,2:T(2,128)}, u32[]{:S(2)}) copy-start(f32[2,512,4096]{1,0,2:T(2,128)} %get-tuple-element.49) | copy-start | bytes 50331652
  832.6 11.8 %copy-start = (f32[2,2,256,8,512]{4,3,2,1,0:T(8,128)S(1)}, f32[2,2,256,8,512]{4,3,2,1,0:T(8,128)}, u32[]{:S(2)}) copy-start(f32[2,2,256,8,512]{4,3,2,1,0:T(8,128)} %copy.177) | copy-start | bytes 50331652
  1032.1 19.4 %copy-start.3 = (f32[2,512,8,512]{3,2,1,0:T(8,128)S(1)}, f32[2,512,8,512]{3,2,1,0:T(8,128)}, u32[]{:S(2)}) copy-start(f32[2,512,8,512]{3,2,1,0:T(8,128)} %copy.240) | copy-start | bytes 50331652
  1079.1 18.7 %copy-start.22 = (s32[4]{0:T(128)S(1)}, s32[4]{0:T(128)}, u32[]{:S(2)}) copy-start(s32[4]{0:T(128)} %param.9) | copy-start | bytes 52
  1079.1 18.7 %copy-start.23 = (f32[256]{0:T(256)S(1)}, f32[256]{0:T(256)}, u32[]{:S(2)}) copy-start(f32[256]{0:T(256)} %get-tuple-element.12) | copy-start | bytes 3076
  1079.1 18.7 %copy-start.24 = (f32[256]{0:T(256)S(1)}, f32[256]{0:T(256)}, u32[]{:S(2)}) copy-start(f32[256]{0:T(256)} %compare_select_fusion.7) | copy-start | bytes 3076
  1079.1 18.7 %copy-start.25 = (f32[4]{0:T(128)S(1)}, f32[4]{0:T(128)}, u32[]{:S(2)}) copy-start(f32[4]{0:T(128)} %get-tuple-element.41) | copy-start | bytes 52
  1079.1 18.7 %copy-start.26 = (f32[4]{0:T(128)S(1)}, f32[4]{0:T(128)}, u32[]{:S(2)}) copy-start(f32[4]{0:T(128)} %get-tuple-element.42) | copy-start | bytes 52
Sparse Core Ops, SparseCore 0:
  458.4 31.4 all-gather.1
  1084.0 6.7 reduce-scatter.3
where the time goes:
time: 1110 us
  matrix products  354 us (32%)
  local copies, waits for them, and re-layouts  310 us (28%)
  waiting for transfers between devices  240 us (22%)
  other arithmetic  161 us (15%)
  blocking collectives  19.2 us (2%)
  between operations  14.1 us (1%)
    dot_general x22, matrix products, exact_einsum(): return jnp.einsum(form, table, operand, precision=lax.Precision.HIGHEST)  354 us
    all_to_all x1, waiting for transfers between devices, on_device(): lax.all_to_all(permuted, 'theta', split_axis=3, concat_axis=2, tiled=True)  217 us
    unnamed x68, local copies, waits for them, and re-layouts  68.2 us
    gather x1, local copies, waits for them, and re-layouts, on_device(): permuted = jnp.take(stacked, owner_map, axis=3)  52.5 us
    unnamed x2, other arithmetic  40.3 us
    dot_general x1, other arithmetic, accumulate(): jnp.einsum('fk,ks,xfks->fxs', row_weights, table, spectrum_block, precisi...  27.6 us
    another operation x3, other arithmetic, on_device(): jnp.stack([jnp.stack([spectrum[0] for spectrum in spectra]), jnp.stack([s...  24 us
  transfers between devices with their start and end apart: 3, of which 3 were waited for; matrix products, arithmetic and copies ran while one was open for 11% of the time, Pallas kernels for 0%

commit v1 on v0

--- a/solution.py
+++ b/solution.py
@@ -1,8 +1,11 @@
+import functools
 import math
 
 import jax
 import jax.numpy as jnp
 from jax import lax
+from jax.experimental import pallas as pl
+from jax.experimental.pallas import tpu as pltpu
 from jax.sharding import PartitionSpec as P
 
 
@@ -94,7 +97,7 @@
     return jnp.stack(terms)
 
 
-def on_device(maps, deltas, spin_rows, ell_index, owner_map, prior):
+def on_device_general(maps, deltas, spin_rows, ell_index, owner_map, prior):
     theta_count = lax.axis_size("theta")
     phi_count = lax.axis_size("phi")
     length = maps.shape[2] * phi_count
@@ -157,7 +160,332 @@
     return jnp.stack([out_real, out_imag], axis=1)
 
 
+ROW_OUTER = 8
+VMEM_LIMIT = 60 * 1024 * 1024
+CODE_TOP = 32767.0
+
+
+def cplx_add(x, y):
+    return tuple(b if a is None else a if b is None else a + b for a, b in zip(x, y))
+
+
+def cplx_sub(x, y):
+    return tuple(
+        (None if b is None else -b) if a is None else a if b is None else a - b
+        for a, b in zip(x, y)
+    )
+
+
+def turn(x, step, count):
+    real, imag = x
+    if step == 0:
+        return x
+    if 4 * step == count:
+        return (imag, None if real is None else -real)
+    cos_v = math.cos(2.0 * math.pi * step / count)
+    sin_v = math.sin(2.0 * math.pi * step / count)
+    if imag is None:
+        return (real * cos_v, real * -sin_v)
+    if 8 * step == count:
+        return ((real + imag) * cos_v, (imag - real) * cos_v)
+    if 8 * step == 3 * count:
+        return ((imag - real) * sin_v, (real + imag) * -sin_v)
+    return (real * cos_v + imag * sin_v, imag * cos_v - real * sin_v)
+
+
+def butterfly(items):
+    count = len(items)
+    if count == 1:
+        return items
+    even, odd = butterfly(items[::2]), butterfly(items[1::2])
+    turned = [turn(x, step, count) for step, x in enumerate(odd)]
+    return [cplx_add(a, b) for a, b in zip(even, turned)] + [
+        cplx_sub(a, b) for a, b in zip(even, turned)
+    ]
+
+
+def split_store(high, low, where, value):
+    top = value.astype(jnp.bfloat16)
+    high[where] = top
+    low[where] = (value - top.astype(jnp.float32)).astype(jnp.bfloat16)
+
+
+def store_matrix(cos_ref, sin_ref, high, low):
+    size = cos_ref.shape[0]
+    first, second = slice(0, size), slice(size, 2 * size)
+    cos_v, sin_v = cos_ref[...], sin_ref[...]
+    split_store(high, low, (first, first), cos_v)
+    split_store(high, low, (first, second), sin_v)
+    split_store(high, low, (second, first), -sin_v)
+    split_store(high, low, (second, second), cos_v)
+
+
+def store_turned(high, low, k, rows, item, cos_t, sin_t):
+    real, imag = item
+    size = real.shape[1]
+    cos_k, sin_k = cos_t[k : k + 1, :], sin_t[k : k + 1, :]
+    if imag is None:
+        out_real, out_imag = real * cos_k, real * -sin_k
+    else:
+        out_real, out_imag = real * cos_k + imag * sin_k, imag * cos_k - real * sin_k
+    split_store(high, low, (k, rows, slice(0, size)), out_real)
+    split_store(high, low, (k, rows, slice(size, 2 * size)), out_imag)
+
+
+def dot_nt(left, right):
+    return lax.dot_general(
+        left, right, (((1,), (1,)), ((), ())), preferred_element_type=jnp.float32
+    )
+
+
+def three_dots(mat_high, mat_low, x_high, x_low, k):
+    high = x_high[k]
+    return (
+        dot_nt(mat_high[...], high) + dot_nt(mat_high[...], x_low[k]) + dot_nt(mat_low[...], high)
+    )
+
+
+def row_kernel(kept, *refs):
+    planes = refs[:-10]
+    cos_b, sin_b, cos_t, sin_t, code_ref, scale_ref, mat_high, mat_low, x_high, x_low = refs[-10:]
+    k = pl.program_id(0)
+    inner = cos_b.shape[0]
+
+    @pl.when(k == 0)
+    def _():
+        store_matrix(cos_b, sin_b, mat_high, mat_low)
+        step_rows = 16
+
+        def chunk(step, carry):
+            rows = pl.ds(pl.multiple_of(step * step_rows, step_rows), step_rows)
+
+            def part(ref, a):
+                return ref[0, rows, a * inner : (a + 1) * inner].astype(jnp.float32)
+
+            items = []
+            for a in range(ROW_OUTER):
+                if len(planes) == 1:
+                    items.append((part(planes[0], a), None))
+                else:
+                    base = part(planes[0], a)
+                    items.append((base * part(planes[1], a), base * part(planes[2], a)))
+            done = butterfly(items)
+            for out in range(kept):
+                store_turned(x_high, x_low, out, rows, done[out], cos_t, sin_t)
+            return carry
+
+        lax.fori_loop(0, planes[0].shape[1] // step_rows, chunk, 0)
+
+    both = three_dots(mat_high, mat_low, x_high, x_low, k)
+    real, imag = both[:inner], both[inner:]
+    top = jnp.max(jnp.maximum(jnp.abs(real), jnp.abs(imag)), axis=1, keepdims=True)
+    top = jnp.maximum(top, 1e-30)
+    factor = CODE_TOP / top
+    code_real = jnp.round(real * factor).astype(jnp.int32)
+    code_imag = jnp.round(imag * factor).astype(jnp.int32)
+    code_ref[0] = (code_real << 16) | (code_imag & 0xFFFF)
+    scale_ref[0] = jnp.broadcast_to(top * (1.0 / CODE_TOP), (inner, 128))
+
+
+def row_call(maps, places, kept, cos_b, sin_b, cos_t, sin_t):
+    rows, length = maps.shape[1:]
+    inner = cos_b.shape[0]
+    whole = lambda shape: pl.BlockSpec(shape, lambda k: (0, 0))
+    plane = lambda place: pl.BlockSpec((1, rows, length), lambda k: (place, 0, 0))
+    return pl.pallas_call(
+        functools.partial(row_kernel, kept),
+        grid=(kept,),
+        in_specs=[plane(place) for place in places]
+        + [whole(cos_b.shape), whole(sin_b.shape), whole(cos_t.shape), whole(sin_t.shape)],
+        out_specs=[
+            pl.BlockSpec((1, inner, rows), lambda k: (k, 0, 0)),
+            pl.BlockSpec((1, inner, 128), lambda k: (k, 0, 0)),
+        ],
+        out_shape=[
+            jax.ShapeDtypeStruct((kept, inner, rows), jnp.int32),
+            jax.ShapeDtypeStruct((kept, inner, 128), jnp.float32),
+        ],
+        scratch_shapes=[
+            pltpu.VMEM((2 * inner, 2 * inner), jnp.bfloat16),
+            pltpu.VMEM((2 * inner, 2 * inner), jnp.bfloat16),
+            pltpu.VMEM((kept, rows, 2 * inner), jnp.bfloat16),
+            pltpu.VMEM((kept, rows, 2 * inner), jnp.bfloat16),
+        ],
+        compiler_params=pltpu.CompilerParams(vmem_limit_bytes=VMEM_LIMIT),
+        cost_estimate=pl.CostEstimate(
+            flops=24 * kept * inner * inner * rows,
+            bytes_accessed=len(places) * rows * length * 2 + kept * inner * (rows + 128) * 4,
+            transcendentals=0,
+        ),
+    )(*([maps] * len(places)), cos_b, sin_b, cos_t, sin_t)
+
+
+def column_kernel(
+    code_ref, sre_ref, sim_ref, table_ref, row_w, cos_b, sin_b, cos_t, sin_t, out_ref,
+    mat_high, mat_low, x_high, x_low, total,
+):
+    k = pl.program_id(0)
+    outer = code_ref.shape[0]
+    slots = code_ref.shape[1]
+    inner = code_ref.shape[2]
+    degrees = table_ref.shape[1]
+
+    @pl.when(k == 0)
+    def _():
+        store_matrix(cos_b, sin_b, mat_high, mat_low)
+        total[...] = jnp.zeros_like(total)
+        step_rows = 16
+
+        def chunk(step, carry):
+            rows = pl.ds(pl.multiple_of(step * step_rows, step_rows), step_rows)
+            sre, sim = sre_ref[rows, :], sim_ref[rows, :]
+            items = []
+            for a in range(outer):
+                code = code_ref[a, rows, :]
+                real = (code >> 16).astype(jnp.float32) * sre[:, a : a + 1]
+                imag = ((code << 16) >> 16).astype(jnp.float32) * sim[:, a : a + 1]
+                items.append((real, imag))
+            for out, item in enumerate(butterfly(items)):
+                store_turned(x_high, x_low, out, rows, item, cos_t, sin_t)
+            return carry
+
+        lax.fori_loop(0, slots // step_rows, chunk, 0)
+
+    both = three_dots(mat_high, mat_low, x_high, x_low, k)
+    real, imag = both[:inner], both[inner:]
+    for degree in range(degrees):
+        weighted = table_ref[0, degree].astype(jnp.float32) * row_w[0, :, degree : degree + 1]
+        for part, value in enumerate((real, imag)):
+            total[2 * degree + part] += jnp.sum(
+                (weighted * value).reshape(inner // 8, 8, slots), axis=0
+            )
+
+    @pl.when(k == outer - 1)
+    def _():
+        out_ref[...] = jnp.sum(total[...], axis=1)
+
+
+def column_call(codes, sre, sim, tables, row_w, cos_b, sin_b, cos_t, sin_t):
+    outer, slots, inner = codes.shape
+    degrees = tables.shape[1]
+    whole = lambda shape: pl.BlockSpec(shape, lambda k: (0,) * len(shape))
+    return pl.pallas_call(
+        column_kernel,
+        grid=(outer,),
+        in_specs=[
+            whole(codes.shape),
+            whole(sre.shape),
+            whole(sim.shape),
+            pl.BlockSpec((1, degrees, inner, slots), lambda k: (k, 0, 0, 0)),
+            pl.BlockSpec((1, inner, degrees), lambda k: (k, 0, 0)),
+            whole(cos_b.shape),
+            whole(sin_b.shape),
+            whole(cos_t.shape),
+            whole(sin_t.shape),
+        ],
+        out_specs=whole((2 * degrees, slots)),
+        out_shape=jax.ShapeDtypeStruct((2 * degrees, slots), jnp.float32),
+        scratch_shapes=[
+            pltpu.VMEM((2 * inner, 2 * inner), jnp.bfloat16),
+            pltpu.VMEM((2 * inner, 2 * inner), jnp.bfloat16),
+            pltpu.VMEM((outer, slots, 2 * inner), jnp.bfloat16),
+            pltpu.VMEM((outer, slots, 2 * inner), jnp.bfloat16),
+            pltpu.VMEM((2 * degrees, 8, slots), jnp.float32),
+        ],
+        compiler_params=pltpu.CompilerParams(vmem_limit_bytes=VMEM_LIMIT),
+        cost_estimate=pl.CostEstimate(
+            flops=24 * outer * inner * inner * slots,
+            bytes_accessed=outer * slots * inner * (4 + 2 * degrees),
+            transcendentals=0,
+        ),
+    )(codes, sre, sim, tables, row_w, cos_b, sin_b, cos_t, sin_t)
+
+
+def trig_tables(row_ids, col_ids, modulus):
+    product = jnp.mod(row_ids[:, None] * col_ids[None, :], modulus)
+    angles = (2.0 * math.pi / modulus) * product.astype(jnp.float32)
+    return jnp.cos(angles), jnp.sin(angles)
+
+
+def signed(ids, length):
+    return jnp.where(ids < length // 2, ids, ids - length)
+
+
+def on_device(maps, deltas, spin_rows, ell_index, owner_map, prior):
+    owners = ("theta", "phi")
+    phi_count = lax.axis_size("phi")
+    length = maps.shape[2] * phi_count
+    outer = lax.axis_size("theta") * phi_count
+    sub_rows = length // outer
+    slots = sub_rows
+    row_inner = length // ROW_OUTER
+    ids = lax.optimization_barrier(jnp.arange(length, dtype=jnp.int32))
+    row_trig = trig_tables(ids[:row_inner], ids[:row_inner], row_inner) + trig_tables(
+        ids[:ROW_OUTER], ids[:row_inner], length
+    )
+    col_trig = trig_tables(ids[:sub_rows], ids[:sub_rows], sub_rows) + trig_tables(
+        ids[:outer], ids[:sub_rows], length
+    )
+    rows = lax.all_to_all(maps, "phi", split_axis=1, concat_axis=2, tiled=True)
+
+    residue = owner_map % ROW_OUTER
+    flipped = residue > ROW_OUTER // 2
+    half_map = jnp.where(flipped, length - owner_map, owner_map)
+    slot_start = (lax.axis_index("theta") * phi_count + lax.axis_index("phi")) * slots
+    own = lambda array: lax.dynamic_slice_in_dim(array, slot_start, slots)
+    own_ids = own(owner_map)
+
+    def spectrum(places, kept, freq):
+        codes, scales = row_call(rows, places, kept, *row_trig)
+        place = (freq % ROW_OUTER) * row_inner + freq // ROW_OUTER
+        table = codes.reshape(kept * row_inner, sub_rows)
+        sorted_codes = table.at[place].get(mode="promise_in_bounds", unique_indices=False)
+        received = lax.all_to_all(
+            sorted_codes.reshape(outer, slots, sub_rows), owners, 0, 0, tiled=True
+        )
+        flat = lax.all_gather(scales[:, :, 0].reshape(-1), owners, axis=0)
+        picks = (own(place)[:, None] == ids[None, : kept * row_inner]).astype(jnp.float32)
+        own_scales = jnp.einsum("am,sm->sa", flat, picks, precision=lax.Precision.HIGHEST)
+        return received, own_scales
+
+    code_scalar, scale_scalar = spectrum((0,), ROW_OUTER // 2 + 1, half_map)
+    code_spin, scale_spin = spectrum((1, 2, 3), ROW_OUTER, owner_map)
+
+    tables = lax.all_to_all(deltas, "phi", split_axis=2, concat_axis=0, tiled=True)
+    degrees = tables.shape[1]
+    tables = tables.reshape(sub_rows, outer, degrees, slots).transpose(1, 2, 0, 3)
+    spins = lax.all_gather(spin_rows, "phi", axis=0, tiled=True).astype(jnp.float32)
+    keep_rows = jnp.abs(signed(ids, length))[:, None] <= ell_index[None, :]
+    row_w = jnp.where(keep_rows[:, None, :], spins, 0.0)
+    row_w = row_w.reshape(sub_rows, outer, 2, degrees).transpose(2, 1, 0, 3)
+
+    mirror = jnp.where(own(flipped), -1.0, 1.0)[:, None]
+    scalar = column_call(
+        code_scalar, scale_scalar, scale_scalar * mirror, tables, row_w[0], *col_trig
+    ).reshape(degrees, 2, slots)
+    spin = column_call(
+        code_spin, scale_spin, scale_spin, tables, row_w[1], *col_trig
+    ).reshape(degrees, 2, slots)
+
+    slot_freq = signed(own_ids, length)
+    ell_float = ell_index.astype(jnp.float32)
+    weight = 2.0 * math.pi / length * jnp.sqrt((2.0 * ell_float + 1.0) / (4.0 * math.pi)) / length
+    keep = jnp.abs(slot_freq)[None, :] <= ell_index[:, None]
+    keep_slots = keep.astype(jnp.float32) * weight[:, None]
+    coupling = (prior * jnp.sqrt(ell_float * (ell_float + 1.0)) / (length // 2))[:, None]
+    inner_real = (-spin[:, 1] - coupling * scalar[:, 0]) * keep_slots
+    inner_imag = (spin[:, 0] - coupling * scalar[:, 1]) * keep_slots
+    turns = jnp.mod(-slot_freq, 4)[None, :]
+    phase_real = jnp.where(turns == 0, 1.0, jnp.where(turns == 2, -1.0, 0.0))
+    phase_imag = jnp.where(turns == 1, 1.0, jnp.where(turns == 3, -1.0, 0.0))
+    out_real = phase_real * inner_real - phase_imag * inner_imag
+    out_imag = phase_real * inner_imag + phase_imag * inner_real
+    return jnp.stack([out_real, out_imag], axis=1)
+
+
 def solution(mesh):
+    owner_count = mesh.shape["theta"] * mesh.shape["phi"]
+    body = on_device if owner_count <= 16 else on_device_general
     placed = (
         P("grp", "theta", "phi"),
         P("phi", None, "theta"),
@@ -167,7 +495,7 @@
         P(),
     )
     return jax.shard_map(
-        on_device,
+        body,
         mesh=mesh,
         in_specs=placed,
         out_specs=P("grp", None, ("theta", "phi")),

time: 1110 us -> 415 us (0.37)
  matrix products: 354 us -> 4.53 us
  waiting for transfers between devices: 240 us -> 44.3 us
  local copies, waits for them, and re-layouts: 310 us -> 142 us
  other arithmetic: 161 us -> 10.5 us
  Pallas kernels: 0 us -> 86.5 us
  blocking collectives: 19.2 us -> 83.2 us
  starting transfers between devices: 7.35 us -> 41.5 us
  between operations: 14.1 us -> 0.22 us
    dot_general x22 -> x2, matrix products: 354 us -> 4.53 us  [spectrum(): jnp.einsum('am,sm->sa', flat, picks, precision=lax.Precision.HIGHEST)]
    all_to_all x1 -> x4, waiting for transfers between devices: 217 us -> 44.3 us  [the longest x2 44.3 us: spectrum(): lax.all_to_all(sorted_codes.reshape(outer, slots, sub_rows), owners, 0, 0...]
    pallas_call x0 -> x4, Pallas kernels: none -> 86.5 us  [the longest x2 46.7 us: column_call(): pl.pallas_call(column_kernel, grid=(outer,), in_specs=[whole(codes.shape)...]
    all_gather x1 -> x3, blocking collectives: 1.84 us -> 83.2 us  [the longest x2 81.1 us: spectrum(): flat = lax.all_gather(scales[:, :, 0].reshape(-1), owners, axis=0)]
    another operation x8 -> x0, local copies, waits for them, and re-layouts: 72.7 us -> none  [the longest x2 18.9 us: on_device(): jnp.stack([spectrum[0] for spectrum in spectra])]
    another operation x6 -> x0, other arithmetic: 49.2 us -> none  [the longest x3 24 us: on_device(): jnp.stack([jnp.stack([spectrum[0] for spectrum in spectra]), jnp.stack([s...]
    unnamed x2 -> x0, other arithmetic: 40.3 us -> none
    unnamed x68 -> x20, local copies, waits for them, and re-layouts: 68.2 us -> 31.3 us
  transfers between devices with their start and end apart: 3 -> 4, of which waited for: 3 -> 1; matrix products, arithmetic and copies ran while one was open for 11% -> 31% of each run, Pallas kernels for 0% -> 15%
where the time goes in v1:
time: 415 us; the launch traced here: 413 us
  local copies, waits for them, and re-layouts  142 us (34%)
  Pallas kernels  86.5 us (21%)
  blocking collectives  83.2 us (20%)
  waiting for transfers between devices  44.3 us (11%)
  starting transfers between devices  41.5 us (10%)
  other arithmetic  10.5 us (3%)
  matrix products  4.53 us (1%)
    all_gather x2, blocking collectives, spectrum(): flat = lax.all_gather(scales[:, :, 0].reshape(-1), owners, axis=0)  81.1 us
    pallas_call x2, Pallas kernels, column_call(): pl.pallas_call(column_kernel, grid=(outer,), in_specs=[whole(codes.shape)...  46.7 us
    all_to_all x2, waiting for transfers between devices, spectrum(): lax.all_to_all(sorted_codes.reshape(outer, slots, sub_rows), owners, 0, 0...  44.3 us
    pallas_call x2, Pallas kernels, row_call(): pl.pallas_call(functools.partial(row_kernel, kept), grid=(kept,), in_spec...  39.8 us
    gather x2, local copies, waits for them, and re-layouts, spectrum(): table.at[place].get(mode='promise_in_bounds', unique_indices=False)  36.2 us
    unnamed x20, local copies, waits for them, and re-layouts  31.3 us
    all_to_all x2, local copies, waits for them, and re-layouts, on_device(): rows = lax.all_to_all(maps, 'phi', split_axis=1, concat_axis=2, tiled=True)  30.9 us
    all_to_all x2, starting transfers between devices, spectrum(): lax.all_to_all(sorted_codes.reshape(outer, slots, sub_rows), owners, 0, 0...  27.4 us
  transfers between devices with their start and end apart: 4, of which 1 were waited for; matrix products, arithmetic and copies ran while one was open for 31% of the time, Pallas kernels for 15%

profile of v1, /device:TPU:0, one launch (start us, length us, event | category | flops | bytes accessed | tf_op | source)
XLA Modules:
  0.0 413.2 jit_solution(10530586881696997783)
XLA Ops:
  0.0 12.2 %copy.39 = bf16[4,512,2048]{2,0,1:T(4,128)(2,1)} copy(bf16[4,512,2048]{2,1,0:T(8,128)(2,1)} %param.6) | data formatting | bytes 16777216 | tf_op args[0]
  12.2 7.1 %all-to-all-start = ((bf16[4,512,2048]{2,0,1:T(4,128)(2,1)}), bf16[4,512,2048]{2,0,1:T(4,128)(2,1)}, u32[]{:S(2)}, u32[]{:S(2)}) async-start(bf16[4,512,2048]{2,0,1:T(4,128)(2,1)} %copy.39), calls=%async_computation | async-start | bytes 16777216 | tf_op jit(solution)/shard_map/all_to_all | solution.py:429
  19.4 0.0 copy-start.2
  19.4 5.9 %fusion.11 = (f32[512,512]{1,0:T(8,128)}, f32[512,512]{1,0:T(8,128)}) fusion(s32[512]{0:T(512)S(1)} %slice.60), kind=kLoop, calls=%fused_computation.24 | loop fusion | flops 3670016 | bytes 2099200 | tf_op jit(solution)/shard_map/sin | solution.py:407
  25.3 0.8 fusion.42
  26.0 0.0 copy-done.4
  26.1 19.0 %copy.41 = bf16[2048,4,512]{0,1,2:T(4,128)(2,1)} copy(bf16[2048,4,512]{2,1,0:T(4,128)(2,1)} %param.7) | data formatting | bytes 16777216 | tf_op args[1]
  45.1 0.0 all-to-all-done
  45.1 6.9 %all-to-all-start.2 = ((bf16[2048,4,512]{0,1,2:T(4,128)(2,1)}), bf16[2048,4,512]{0,1,2:T(4,128)(2,1)}, u32[]{:S(2)}, u32[]{:S(2)}) async-start(bf16[2048,4,512]{0,1,2:T(4,128)(2,1)} %copy.41), calls=%async_computation.2 | async-start | bytes 16777216 | tf_op jit(solution)/shard_map/all_to_all | solution.py:454
  52.0 16.4 %copy.68 = bf16[4,2,256,2048]{3,1,2,0:T(2,128)(2,1)} copy(bf16[4,2,256,2048]{3,0,2,1:T(4,128)(2,1)} %bitcast) | data formatting | bytes 16777216 | tf_op jit(solution)/shard_map/all_to_all | solution.py:429
  68.5 14.5 %all_to_all.33.refs_0_.refs_1_.refs_2_ = bf16[4,256,4096]{2,1,0:T(8,128)(2,1)} reshape(bf16[4,256,2,2048]{3,2,1,0:T(2,128)(2,1)} %bitcast.32) | data formatting | bytes 16777216 | tf_op jit(solution)/shard_map/all_to_all | solution.py:429
  83.0 24.5 %shard_map.64 = (s32[8,512,256]{2,1,0:T(8,128)}, f32[8,512,128]{2,1,0:T(8,128)}) custom-call(bf16[4,256,4096]{2,1,0:T(8,128)(2,1)} %all_to_all.33.refs_0_.refs_1_.refs_2_, bf16[4,256,4096]{2,1,0:T(8,128)(2,1)} %all_to_all.33.refs_0_.refs_1_.refs_2_, bf16[4,256,4096]{2,1,0:T(8,128)(2,1)} %all_to_all.33.refs_0_.refs_1_.refs_2_, ...), custom_call_target="tpu_custom_call" | custom-call | flops 12884901888 | bytes 12582912 | tf_op jit(solution)/shard_map/pallas_call | solution.py:295
  107.5 18.3 %gather_fusion = s32[4096,256]{1,0:T(8,128)} fusion(s32[4096,256]{1,0:T(8,128)} %bitcast.31, s32[4096]{0:T(1024)S(1)} %get-tuple-element.18), kind=kCustom, calls=%fused_computation | custom fusion | bytes 8404992 | tf_op jit(solution)/shard_map/gather | solution.py:442
  125.8 0.0 all-to-all-done.2
  125.8 7.6 %all-to-all-start.1 = ((s32[16,256,256]{2,1,0:T(8,128)}), s32[16,256,256]{2,1,0:T(8,128)}, u32[]{:S(2)}, u32[]{:S(2)}) async-start(s32[16,256,256]{2,1,0:T(8,128)} %bitcast.36), calls=%async_computation.1 | async-start | bytes 8388608 | tf_op jit(solution)/shard_map/all_to_all | solution.py:443
  133.4 15.3 %shard_map.66 = (s32[5,512,256]{2,1,0:T(8,128)}, f32[5,512,128]{2,1,0:T(8,128)}) custom-call(bf16[4,256,4096]{2,1,0:T(8,128)(2,1)} %all_to_all.33.refs_0_.refs_1_.refs_2_, f32[512,512]{1,0:T(8,128)} %get-tuple-element.29.refs_3_.refs_1_, f32[512,512]{1,0:T(8,128)} %get-tuple-element.28.refs_4_.refs_2_, f32[8,512]{1,0:T(8,128)} %get-tuple-element.27.refs_5_.refs_3_, ...), custom_call_target="tpu_custom_call" | custom-call | flops 8053063680 | bytes 6029312 | tf_op jit(solution)/shard_map/pallas_call | solution.py:295
  148.7 17.9 %gather_fusion.1 = s32[4096,256]{1,0:T(8,128)} fusion(s32[2560,256]{1,0:T(8,128)} %bitcast.30, s32[4096]{0:T(1024)S(1)} %get-tuple-element.24), kind=kCustom, calls=%fused_computation.1 | custom fusion | bytes 8404992 | tf_op jit(solution)/shard_map/gather | solution.py:442
  166.6 44.3 %all-to-all-done.1.code_ref = s32[16,256,256]{2,1,0:T(8,128)} async-done(((s32[16,256,256]{2,1,0:T(8,128)}), s32[16,256,256]{2,1,0:T(8,128)}, u32[]{:S(2)}, u32[]{:S(2)}) %all-to-all-start.1) | async-done | bytes 4194336 | tf_op jit(solution)/shard_map/all_to_all | solution.py:443
  210.9 19.8 %all-to-all-start.3 = ((s32[16,256,256]{2,1,0:T(8,128)}), s32[16,256,256]{2,1,0:T(8,128)}, u32[]{:S(2)}, u32[]{:S(2)}) async-start(s32[16,256,256]{2,1,0:T(8,128)} %bitcast.35), calls=%async_computation.3 | async-start | bytes 8388608 | tf_op jit(solution)/shard_map/all_to_all | solution.py:443
  230.7 0.0 copy-start.1
  230.8 0.1 dynamic_slice.13
  230.9 0.1 dynamic_slice.14
  230.9 2.2 all_gather.10
  233.1 0.1 broadcast_compare_fusion
  233.3 0.4 reshape.180
  233.6 5.0 %copy.45 = f32[256,16,2,4]{3,0,1,2:T(8,128)} copy(f32[256,16,2,4]{1,0,3,2:T(8,128)S(1)} %reshape.180) | data formatting | bytes 262144 | tf_op jit(solution)/shard_map/reshape | solution.py:460
  238.6 1.7 slice_reduce_fusion.1
  240.4 0.6 slice_reduce_fusion
  241.0 11.2 %copy.42 = bf16[2048,4,512]{0,2,1:T(8,128)(2,1)} copy(bf16[2048,4,512]{0,1,2:T(4,128)(2,1)} %all-to-all-done.2) | data formatting | bytes 16777216 | tf_op jit(solution)/shard_map/all_to_all | solution.py:454
  252.3 11.4 %copy.43 = bf16[2,2048,4,256]{3,1,0,2:T(8,128)(2,1)} copy(bf16[2,2048,4,256]{1,3,0,2:T(8,128)(2,1)} %bitcast.33) | data formatting | bytes 16777216 | tf_op jit(solution)/shard_map/all_to_all | solution.py:454
  263.7 9.7 %copy.67 = bf16[256,16,4,256]{3,0,2,1:T(8,128)(2,1)} copy(bf16[256,16,4,256]{3,1,0,2:T(8,128)(2,1)} %bitcast.34) | data formatting | bytes 16777216 | tf_op jit(solution)/shard_map/reshape | solution.py:456
  273.4 44.9 %all-gather.1 = f32[16,1,2560]{2,1,0:T(1,128)S(1)} all-gather(f32[1,1,2560]{2,1,0:T(1,128)S(1)} %reshape.205), channel_id=1, replica_groups=mesh['grp'=2,'theta'=8,'phi'=2] {'theta','phi'}, dimensions={0}, use_global_device_ids=true | all-gather | bytes 174080 | tf_op jit(solution)/shard_map/all_gather | solution.py:446
  318.4 0.1 fusion.52
  318.5 0.1 dynamic-slice_select_fusion
  318.5 0.1 compare_select_fusion.10
  318.6 36.1 %all-gather = f32[16,1,4096]{2,1,0:T(1,128)S(1)} all-gather(f32[1,1,4096]{2,1,0:T(1,128)S(1)} %reshape.203), channel_id=1, replica_groups=mesh['grp'=2,'theta'=8,'phi'=2] {'theta','phi'}, dimensions={0}, use_global_device_ids=true | all-gather | bytes 278528 | tf_op jit(solution)/shard_map/all_gather | solution.py:446
  354.8 0.8 fusion.40
  355.6 2.6 fusion.sre_ref.sim_ref
  358.1 1.9 broadcast_multiply_fusion
  360.1 1.9 fusion.20
  362.0 2.3 slice_bitcast_fusion.1
  364.3 23.4 %shard_map.65 = f32[8,256]{1,0:T(8,128)} custom-call(s32[16,256,256]{2,1,0:T(8,128)} %all-to-all-done.1.code_ref, f32[256,16]{1,0:T(8,128)} %fusion.sre_ref.sim_ref, f32[256,16]{1,0:T(8,128)} %fusion.sre_ref.sim_ref, bf16[16,4,256,256]{3,2,1,0:T(8,128)(2,1)} %bitcast.38, f32[16,256,4]{2,1,0:T(8,128)} %get-tuple-element.22.row_w, ...), custom_call_target="tpu_custom_call" | custom-call | flops 6442450944 | bytes 12582912 | tf_op jit(solution)/shard_map/pallas_call | solution.py:372
  387.7 0.7 reshape.181
  388.4 0.0 all-to-all-done.3.code_ref
  388.4 23.3 %shard_map.67 = f32[8,256]{1,0:T(8,128)} custom-call(s32[16,256,256]{2,1,0:T(8,128)} %all-to-all-done.3.code_ref, f32[256,16]{1,0:T(8,128)} %get-tuple-element.37.sre_ref, f32[256,16]{1,0:T(8,128)} %get-tuple-element.36.sim_ref, bf16[16,4,256,256]{3,2,1,0:T(8,128)(2,1)} %bitcast.39, f32[16,256,4]{2,1,0:T(8,128)} %get-tuple-element.23.row_w, ...), custom_call_target="tpu_custom_call" | custom-call | flops 6442450944 | bytes 12582912 | tf_op jit(solution)/shard_map/pallas_call | solution.py:372
  411.7 0.7 reshape.184
  412.4 0.1 multiply_subtract_fusion
  412.5 0.6 pad_maximum_fusion
  (30 shorter events, 0.2 us)
Async XLA Ops:
  12.2 13.8 %copy-start.4 = (s32[4096]{0:T(1024)S(1)}, s32[4096]{0:T(1024)}, u32[]{:S(2)}) copy-start(s32[4096]{0:T(1024)} %param.10) | copy-start | bytes 49156
  12.2 32.9 %all-to-all-start = ((bf16[4,512,2048]{2,0,1:T(4,128)(2,1)}), bf16[4,512,2048]{2,0,1:T(4,128)(2,1)}, u32[]{:S(2)}, u32[]{:S(2)}) async-start(bf16[4,512,2048]{2,0,1:T(4,128)(2,1)} %copy.39), calls=%async_computation | async-start | bytes 16777216 | tf_op jit(solution)/shard_map/all_to_all | solution.py:429
  19.4 213.7 %copy-start.2 = (s32[4096]{0:T(1024)}, s32[4096]{0:T(1024)S(1)}, u32[]{:S(2)}) copy-start(s32[4096]{0:T(1024)S(1)} %iota.3) | copy-start | bytes 49156
  45.1 80.7 %all-to-all-start.2 = ((bf16[2048,4,512]{0,1,2:T(4,128)(2,1)}), bf16[2048,4,512]{0,1,2:T(4,128)(2,1)}, u32[]{:S(2)}, u32[]{:S(2)}) async-start(bf16[2048,4,512]{0,1,2:T(4,128)(2,1)} %copy.41), calls=%async_computation.2 | async-start | bytes 16777216 | tf_op jit(solution)/shard_map/all_to_all | solution.py:454
  125.8 85.1 %all-to-all-start.1 = ((s32[16,256,256]{2,1,0:T(8,128)}), s32[16,256,256]{2,1,0:T(8,128)}, u32[]{:S(2)}, u32[]{:S(2)}) async-start(s32[16,256,256]{2,1,0:T(8,128)} %bitcast.36), calls=%async_computation.1 | async-start | bytes 8388608 | tf_op jit(solution)/shard_map/all_to_all | solution.py:443
  210.9 20.0 %copy-start.5 = (bf16[2048,2,4]{0,2,1:T(4,128)(2,1)S(1)}, bf16[2048,2,4]{0,2,1:T(4,128)(2,1)}, u32[]{:S(2)}) copy-start(bf16[2048,2,4]{0,2,1:T(4,128)(2,1)} %param.8) | copy-start | bytes 98308
  210.9 22.2 %copy-start.6 = (s32[4]{0:T(128)S(1)}, s32[4]{0:T(128)}, u32[]{:S(2)}) copy-start(s32[4]{0:T(128)} %param.9) | copy-start | bytes 52
  210.9 177.5 %all-to-all-start.3 = ((s32[16,256,256]{2,1,0:T(8,128)}), s32[16,256,256]{2,1,0:T(8,128)}, u32[]{:S(2)}, u32[]{:S(2)}) async-start(s32[16,256,256]{2,1,0:T(8,128)} %bitcast.35), calls=%async_computation.3 | async-start | bytes 8388608 | tf_op jit(solution)/shard_map/all_to_all | solution.py:443
  230.7 9.6 %copy-start.1 = (f32[8,512,128]{2,1,0:T(8,128)S(1)}, f32[8,512,128]{2,1,0:T(8,128)}, u32[]{:S(2)}) copy-start(f32[8,512,128]{2,1,0:T(8,128)} %get-tuple-element.10) | copy-start | bytes 6291460
  263.7 91.0 %copy-start.7 = (f32[4]{0:T(128)S(1)}, f32[4]{0:T(128)}, u32[]{:S(2)}) copy-start(f32[4]{0:T(128)} %param.11) | copy-start | bytes 52
  263.7 91.1 %slice-start = ((s32[4096]{0:T(1024)}), s32[16]{0:T(128)S(1)}, s32[]{:S(2)}) async-start(s32[4096]{0:T(1024)} %copy-done.2), calls=%async_computation.4 | async-start | bytes 1024 | tf_op jit(solution)/shard_map/slice | solution.py:427
  263.7 91.8 %copy-start.3 = (s32[4096]{0:T(1024)S(1)}, s32[4096]{0:T(1024)}, u32[]{:S(2)}) copy-start(s32[4096]{0:T(1024)} %copy-done.2) | copy-start | bytes 49156
  263.7 94.4 %slice-start.1 = ((s32[4096]{0:T(1024)}), s32[2560]{0:T(1024)S(1)}, s32[]{:S(2)}) async-start(s32[4096]{0:T(1024)} %copy-done.2), calls=%async_computation.5 | async-start | bytes 24576 | tf_op jit(solution)/shard_map/slice | solution.py:447
  273.4 88.6 %copy-start = (f32[256,16,2,4]{3,0,1,2:T(8,128)S(1)}, f32[256,16,2,4]{3,0,1,2:T(8,128)}, u32[]{:S(2)}) copy-start(f32[256,16,2,4]{3,0,1,2:T(8,128)} %copy.45) | copy-start | bytes 393220
